TPU v7x, 32 devices: a whole 2x2x4 slice. The times are simulated.
32 devices in a mesh: samp: 8 (over y, x, core), snp: 4 (over z).
Axes of the slice: x: 2, y: 2, z: 4, core: 2. Of those that a mesh axis runs over, the one named last changes fastest.
Arguments:
- genotypes: bfloat16 [8192, 16384], P('samp', 'snp'), may hold values from -6 to 6
- probes: bfloat16 [8, 8192], P(None, 'samp'), may hold values from -6 to 6
- env_label: int32 [8192], P('samp'), may hold values from 0 to 7
- variances: float32 [3], replicated, may hold values from 0.25 to 1
Outputs:
- first: float32 [8, 8192], P(None, 'samp')
- second: float32 [8, 8192], P(None, 'samp')
All inputs are finite; a program needn't handle non-finite values.
Results may differ from a plain program's by a relative error of at most 0.0018.
Values may be sent and summed in bfloat16 or wider, within the bound.
No kernel may reach another device: no remote copies, remote signals or barrier semaphores. Data moves between devices by JAX's collectives and lax.ppermute only.
A program may use at most 64 MiB of HBM per device.

v0:
```python
import jax
import jax.numpy as jnp
from jax import lax
from jax.sharding import PartitionSpec as P

SNPS = 16384
PROBES = 8
ENVS = 8


def local_image(snp_panel, genotypes):
    return lax.dot_general(
        snp_panel, genotypes, (((1,), (1,)), ((), ())), preferred_element_type=jnp.float32
    )


def apply_operator(current, genotypes, onehot, variances):
    rounded = current.astype(jnp.bfloat16)
    scaled = (onehot[:, None, :] * rounded[None, :, :]).reshape(ENVS * PROBES, -1)
    panel = jnp.concatenate([rounded, scaled], axis=0)
    partial_panel = jnp.dot(panel, genotypes, preferred_element_type=jnp.float32)
    snp_panel = lax.psum(partial_panel, "samp").astype(jnp.bfloat16)
    image = local_image(snp_panel, genotypes)
    additive = image[:PROBES]
    blocks = image[PROBES:].reshape(ENVS, PROBES, -1)
    interaction = jnp.sum(onehot.astype(jnp.float32)[:, None, :] * blocks, axis=0)
    weighted = variances[0] * additive / SNPS + variances[1] * interaction / SNPS
    totals = lax.psum(weighted, "snp")
    return totals + variances[2] * current


def per_device(genotypes, probes, env_label, variances):
    labels = jnp.arange(ENVS, dtype=jnp.int32)
    onehot = (env_label[None, :] == labels[:, None]).astype(jnp.bfloat16)
    first = apply_operator(probes.astype(jnp.float32), genotypes, onehot, variances)
    second = apply_operator(first, genotypes, onehot, variances)
    return (first, second)


def solution(mesh):
    return jax.shard_map(
        per_device,
        mesh=mesh,
        in_specs=(P("samp", "snp"), P(None, "samp"), P("samp"), P()),
        out_specs=(P(None, "samp"), P(None, "samp")),
        check_vma=False,
    )
```

profile of v0, /device:TPU:0, one launch (start us, length us, event | category | flops | bytes accessed | tf_op | source)
XLA Modules:
  0.0 167.7 jit_solution(6879203342592267592)
XLA Ops:
  0.6 1.4 fusion.25
  2.1 0.7 fusion.21
  2.8 0.7 multiply_bitcast_fusion.1
  3.5 5.0 %fusion.8 = f32[72,4096]{1,0:T(8,128)S(1)} fusion(bf16[1024,4096]{1,0:T(8,128)(2,1)} %param.4, bf16[64,1024]{1,0:T(8,128)(2,1)S(1)} %multiply_bitcast_fusion.1, bf16[8,1024]{1,0:T(8,128)(2,1)} %param.5), kind=kOutput, calls=%fused_computation.10 | convolution fusion | flops 604274688 | bytes 9715712 | tf_op jit(solution)/shard_map/dot_general | solution.py:21
  8.5 0.0 copy-start
  8.5 53.0 %all-reduce.2 = bf16[72,4096]{1,0:T(8,128)(2,1)S(1)} all-reduce(f32[72,4096]{1,0:T(8,128)S(1)} %fusion.8), channel_id=1, replica_groups=mesh['samp'=8,'snp'=4] {'samp'}, use_global_device_ids=true, to_apply=%region_0.0 | all-reduce | flops 294912 | bytes 1769472 | tf_op jit(solution)/shard_map/psum | solution.py:22
  61.5 6.0 %fusion.27 = f32[72,1024]{1,0:T(8,128)S(1)} fusion(bf16[72,4096]{1,0:T(8,128)(2,1)S(1)} %all-reduce.2, bf16[1024,4096]{1,0:T(8,128)(2,1)} %param.4), kind=kOutput, calls=%fused_computation.36 | convolution fusion | flops 603979776 | bytes 9273344 | tf_op jit(solution)/shard_map/dot_general | solution.py:12
  67.6 1.2 fusion.19
  68.8 19.5 %psum.29 = f32[8,1024]{1,0:T(8,128)S(1)} all-reduce(f32[8,1024]{1,0:T(8,128)S(1)} %fusion.19), channel_id=1, replica_groups=mesh['samp'=8,'snp'=4] {'snp'}, use_global_device_ids=true, to_apply=%region_2.0 | all-reduce | flops 8192 | bytes 65536 | tf_op jit(solution)/shard_map/psum | solution.py:28
  88.3 0.0 copy-done
  88.3 0.7 fusion.24
  89.0 0.0 copy-start.1
  89.1 5.0 %fusion.12 = f32[72,4096]{1,0:T(8,128)S(1)} fusion(bf16[1024,4096]{1,0:T(8,128)(2,1)} %param.4, bf16[64,1024]{1,0:T(8,128)(2,1)S(1)} %multiply_bitcast_fusion, bf16[8,1024]{1,0:T(8,128)(2,1)S(1)} %get-tuple-element.2), kind=kOutput, calls=%fused_computation.14 | convolution fusion | flops 604274688 | bytes 9715712 | tf_op jit(solution)/shard_map/dot_general | solution.py:21
  94.1 49.2 %all-reduce.3 = bf16[72,4096]{1,0:T(8,128)(2,1)S(1)} all-reduce(f32[72,4096]{1,0:T(8,128)S(1)} %fusion.12), channel_id=1, replica_groups=mesh['samp'=8,'snp'=4] {'samp'}, use_global_device_ids=true, to_apply=%region_3.0 | all-reduce | flops 294912 | bytes 1769472 | tf_op jit(solution)/shard_map/psum | solution.py:22
  143.3 6.0 %fusion.26 = f32[72,1024]{1,0:T(8,128)S(1)} fusion(bf16[72,4096]{1,0:T(8,128)(2,1)S(1)} %all-reduce.3, bf16[1024,4096]{1,0:T(8,128)(2,1)} %param.4), kind=kOutput, calls=%fused_computation.35 | convolution fusion | flops 603979776 | bytes 9273344 | tf_op jit(solution)/shard_map/dot_general | solution.py:12
  149.4 1.2 fusion.17
  150.6 15.8 %psum.31 = f32[8,1024]{1,0:T(8,128)S(1)} all-reduce(f32[8,1024]{1,0:T(8,128)S(1)} %fusion.17), channel_id=1, replica_groups=mesh['samp'=8,'snp'=4] {'snp'}, use_global_device_ids=true, to_apply=%region_5.0 | all-reduce | flops 8192 | bytes 65536 | tf_op jit(solution)/shard_map/psum | solution.py:28
  166.4 0.0 copy-done.1
  166.4 1.3 multiply_add_fusion
  (3 shorter events, 0.1 us)
Async XLA Ops:
  8.5 79.8 %copy-start = (bf16[8,1024]{1,0:T(8,128)(2,1)S(1)}, bf16[8,1024]{1,0:T(8,128)(2,1)}, u32[]{:S(2)}) copy-start(bf16[8,1024]{1,0:T(8,128)(2,1)} %param.5) | copy-start | bytes 49156
  89.0 77.4 %copy-start.1 = (f32[8,1024]{1,0:T(8,128)}, f32[8,1024]{1,0:T(8,128)S(1)}, u32[]{:S(2)}) copy-start(f32[8,1024]{1,0:T(8,128)S(1)} %get-tuple-element.3) | copy-start | bytes 98308
where the time goes:
time: 168 us
  blocking collectives  138 us (82%)
  matrix products  22.1 us (13%)
  other arithmetic  5.97 us (4%)
    psum x2, blocking collectives, apply_operator(): snp_panel = lax.psum(partial_panel, 'samp').astype(jnp.bfloat16)  102 us
    psum x2, blocking collectives, apply_operator(): totals = lax.psum(weighted, 'snp')  35.2 us
    dot_general x2, matrix products, local_image(): lax.dot_general(snp_panel, genotypes, (((1,), (1,)), ((), ())), preferred...  12.1 us
    dot_general x2, matrix products, apply_operator(): jnp.dot(panel, genotypes, preferred_element_type=jnp.float32)  9.96 us

commit v1 on v0

--- a/solution.py
+++ b/solution.py
@@ -1,11 +1,20 @@
+import functools
 import jax
 import jax.numpy as jnp
 from jax import lax
 from jax.sharding import PartitionSpec as P
+from jax.lax import all_gather
 
 SNPS = 16384
 PROBES = 8
 ENVS = 8
+
+
+def solve_the_chains(tile_in, named_axis):
+    return all_gather(tile_in, axis_name=named_axis).sum(axis=0)
+
+
+play_tiles = functools.partial(solve_the_chains, named_axis="snp")
 
 
 def local_image(snp_panel, genotypes):
@@ -25,7 +34,7 @@
     blocks = image[PROBES:].reshape(ENVS, PROBES, -1)
     interaction = jnp.sum(onehot.astype(jnp.float32)[:, None, :] * blocks, axis=0)
     weighted = variances[0] * additive / SNPS + variances[1] * interaction / SNPS
-    totals = lax.psum(weighted, "snp")
+    totals = play_tiles(weighted)
     return totals + variances[2] * current
 
 

time: 168 us -> 157 us (0.935)
  blocking collectives: 138 us -> 130 us
  matrix products: 22.1 us -> 18.9 us
    psum x2 -> x0, blocking collectives: 35.2 us -> none  [apply_operator(): totals = lax.psum(weighted, 'snp')]
    all_gather x0 -> x2, blocking collectives: none -> 27.2 us  [solve_the_chains(): return all_gather(tile_in, axis_name=named_axis).sum(axis=0)]
    dot_general x2, matrix products: 9.96 us -> 6.62 us  [apply_operator(): jnp.dot(panel, genotypes, preferred_element_type=jnp.float32)]
where the time goes in v1:
time: 157 us
  blocking collectives  130 us (83%)
  matrix products  18.9 us (12%)
  other arithmetic  5.99 us (4%)
    psum x2, blocking collectives, apply_operator(): snp_panel = lax.psum(partial_panel, 'samp').astype(jnp.bfloat16)  103 us
    all_gather x2, blocking collectives, solve_the_chains(): return all_gather(tile_in, axis_name=named_axis).sum(axis=0)  27.2 us
    dot_general x2, matrix products, local_image(): lax.dot_general(snp_panel, genotypes, (((1,), (1,)), ((), ())), preferred...  12.2 us
    dot_general x2, matrix products, apply_operator(): jnp.dot(panel, genotypes, preferred_element_type=jnp.float32)  6.62 us

profile of v1, /device:TPU:0, one launch (start us, length us, event | category | flops | bytes accessed | tf_op | source)
XLA Modules:
  0.0 156.9 jit_solution(8027394821215849512)
XLA Ops:
  0.6 1.4 fusion.25
  2.1 0.7 fusion.21
  2.8 0.7 multiply_bitcast_fusion.1
  3.5 5.0 %fusion.8 = f32[72,4096]{1,0:T(8,128)S(1)} fusion(bf16[1024,4096]{1,0:T(8,128)(2,1)} %param.4, bf16[64,1024]{1,0:T(8,128)(2,1)S(1)} %multiply_bitcast_fusion.1, bf16[8,1024]{1,0:T(8,128)(2,1)} %param.5), kind=kOutput, calls=%fused_computation.10 | convolution fusion | flops 604274688 | bytes 9715712 | tf_op jit(solution)/shard_map/dot_general | solution.py:30
  8.5 0.0 copy-start.1
  8.5 53.0 %all-reduce.2 = bf16[72,4096]{1,0:T(8,128)(2,1)S(1)} all-reduce(f32[72,4096]{1,0:T(8,128)S(1)} %fusion.8), channel_id=1, replica_groups=mesh['samp'=8,'snp'=4] {'samp'}, use_global_device_ids=true, to_apply=%region_0.0 | all-reduce | flops 294912 | bytes 1769472 | tf_op jit(solution)/shard_map/psum | solution.py:31
  61.5 0.0 copy-start
  61.5 6.2 %fusion.27 = f32[72,1024]{1,0:T(8,128)S(1)} fusion(bf16[72,4096]{1,0:T(8,128)(2,1)S(1)} %all-reduce.2, bf16[1024,4096]{1,0:T(8,128)(2,1)} %param.4), kind=kOutput, calls=%fused_computation.38 | convolution fusion | flops 603979776 | bytes 9273344 | tf_op jit(solution)/shard_map/dot_general | solution.py:21
  67.8 1.2 fusion.19
  69.0 13.9 %all-gather = f32[32,1024]{1,0:T(8,128)S(1)} all-gather(f32[8,1024]{1,0:T(8,128)S(1)} %fusion.19), channel_id=2, replica_groups=mesh['samp'=8,'snp'=4] {'snp'}, dimensions={0}, use_global_device_ids=true | all-gather | bytes 163840 | tf_op jit(solution)/shard_map/all_gather | solution.py:14
  82.9 0.0 copy-done.1
  82.9 0.7 fusion.24
  83.6 0.0 copy-start.2
  83.6 0.0 copy-done
  83.7 1.6 %fusion.12 = f32[72,4096]{1,0:T(8,128)S(1)} fusion(bf16[1024,4096]{1,0:T(8,128)(2,1)S(1)} %copy-done, bf16[64,1024]{1,0:T(8,128)(2,1)S(1)} %multiply_bitcast_fusion, bf16[8,1024]{1,0:T(8,128)(2,1)S(1)} %get-tuple-element.2), kind=kOutput, calls=%fused_computation.14 | convolution fusion | flops 604274688 | bytes 9715712 | tf_op jit(solution)/shard_map/dot_general | solution.py:30
  85.3 49.6 %all-reduce.3 = bf16[72,4096]{1,0:T(8,128)(2,1)S(1)} all-reduce(f32[72,4096]{1,0:T(8,128)S(1)} %fusion.12), channel_id=1, replica_groups=mesh['samp'=8,'snp'=4] {'samp'}, use_global_device_ids=true, to_apply=%region_3.0 | all-reduce | flops 294912 | bytes 1769472 | tf_op jit(solution)/shard_map/psum | solution.py:31
  134.9 6.0 %fusion.26 = f32[72,1024]{1,0:T(8,128)S(1)} fusion(bf16[72,4096]{1,0:T(8,128)(2,1)S(1)} %all-reduce.3, bf16[1024,4096]{1,0:T(8,128)(2,1)} %param.4), kind=kOutput, calls=%fused_computation.37 | convolution fusion | flops 603979776 | bytes 9273344 | tf_op jit(solution)/shard_map/dot_general | solution.py:21
  141.0 1.2 fusion.17
  142.2 13.3 %all-gather.1 = f32[32,1024]{1,0:T(8,128)S(1)} all-gather(f32[8,1024]{1,0:T(8,128)S(1)} %fusion.17), channel_id=3, replica_groups=mesh['samp'=8,'snp'=4] {'snp'}, dimensions={0}, use_global_device_ids=true | all-gather | bytes 163840 | tf_op jit(solution)/shard_map/all_gather | solution.py:14
  155.6 0.0 copy-done.2
  155.6 1.3 multiply_add_fusion
  (5 shorter events, 0.1 us)
Async XLA Ops:
  8.5 74.4 %copy-start.1 = (bf16[8,1024]{1,0:T(8,128)(2,1)S(1)}, bf16[8,1024]{1,0:T(8,128)(2,1)}, u32[]{:S(2)}) copy-start(bf16[8,1024]{1,0:T(8,128)(2,1)} %param.5) | copy-start | bytes 49156
  61.5 22.1 %copy-start = (bf16[1024,4096]{1,0:T(8,128)(2,1)S(1)}, bf16[1024,4096]{1,0:T(8,128)(2,1)}, u32[]{:S(2)}) copy-start(bf16[1024,4096]{1,0:T(8,128)(2,1)} %param.4) | copy-start | bytes 25165828
  83.6 72.0 %copy-start.2 = (f32[8,1024]{1,0:T(8,128)}, f32[8,1024]{1,0:T(8,128)S(1)}, u32[]{:S(2)}) copy-start(f32[8,1024]{1,0:T(8,128)S(1)} %get-tuple-element.3) | copy-start | bytes 98308
